TPU v7x, 32 devices: a whole 2x2x4 slice. The times are simulated.
32 devices in a mesh: dp: 8 (over z, y), mp: 4 (over x, core).
Axes of the slice: x: 2, y: 2, z: 4, core: 2. Of those that a mesh axis runs over, the one named last changes fastest.
Arguments:
- tokens: bfloat16 [8, 1024, 1280], P('dp', 'mp'), may hold values from -6 to 6
- sizes: float32 [8, 1024], P('dp'), may hold values from 1 to 8
- ln1_gain: float32 [1280], replicated, may hold values from 0.25 to 1.75
- qkv_weight: bfloat16 [3, 1280, 1280], P(None, 'dp', 'mp'), may hold values from -0.15625 to 0.15625
- proj_weight: bfloat16 [1280, 1280], P('mp', 'dp'), may hold values from -0.15625 to 0.15625
- ln2_gain: float32 [1280], replicated, may hold values from 0.25 to 1.75
- fc1_weight: bfloat16 [1280, 5120], P('dp', 'mp'), may hold values from -0.15625 to 0.15625
- fc1_bias: float32 [5120], P('mp'), may hold values from -3 to 3
- fc2_weight: bfloat16 [5120, 1280], P('mp', 'dp'), may hold values from -0.078125 to 0.078125
- pair_source: int32 [8, 16], P('dp'), may hold values from 0 to 1022, as said below
- pair_target: int32 [8, 16], P('dp'), may hold values from 1 to 1023, as said below
- kept_order: int32 [8, 1008], P('dp'), may hold values from 0 to 1023, as said below
Outputs:
- merged_out: bfloat16 [8, 1008, 1280], P('dp', 'mp')
Inputs may be any that keep to these rules, and one draw needn't show every extreme that they name: `pair_source`: in each image the 16 entries are distinct even token indices. `pair_target`: odd token indices; several sources may join the same target. `kept_order`: in each image every token index that is not in pair_source appears exactly once.
All inputs are finite; a program needn't handle non-finite values.
Results may differ from a plain program's by a relative error of at most 0.017.
Values may be sent and summed in bfloat16 or wider, within the bound.
A program may use at most 64 MiB of HBM per device.

v0:
```python
import math
import jax
import jax.numpy as jnp
from jax import lax
from jax.sharding import PartitionSpec as P

D = 1280
HEADS = 16


def layer_norm(values, gain):
    center = values - jnp.mean(values, axis=-1, keepdims=True)
    spread = jnp.mean(center * center, axis=-1, keepdims=True)
    return center * lax.rsqrt(spread + 1e-06) * gain


def merge_rows(total, order_rows, source_ids, target_ids):
    kept_rows = jnp.take_along_axis(total, order_rows[:, :, None], axis=1)
    source_rows = jnp.take_along_axis(total, source_ids[:, :, None], axis=1)
    joins = (order_rows[:, :, None] == target_ids[:, None, :]).astype(jnp.float32)
    return kept_rows + jnp.einsum(
        "icr,ird->icd", joins, source_rows, precision=lax.Precision.HIGHEST
    )


def shards(
    tokens,
    sizes,
    ln1_gain,
    qkv_weight,
    proj_weight,
    ln2_gain,
    fc1_weight,
    fc1_bias,
    fc2_weight,
    pair_source,
    pair_target,
    kept_order,
):
    images, own_tokens, width = tokens.shape
    length = sizes.shape[1]
    kept_total = kept_order.shape[1]
    devices_mp = lax.axis_size("mp")
    own_start = lax.axis_index("mp") * own_tokens
    head_size = D // HEADS
    base = tokens.astype(jnp.float32)
    normed = layer_norm(base, ln1_gain).astype(jnp.bfloat16)
    whole = lax.all_gather(normed, "mp", axis=1, tiled=True)
    local_width = qkv_weight.shape[2]
    columns = whole
    projected = jnp.einsum(
        "ind,cdf->cinf",
        columns,
        lax.all_gather(qkv_weight, "dp", axis=1, tiled=True),
        preferred_element_type=jnp.float32,
    ).astype(jnp.bfloat16)
    local_heads = local_width // head_size
    shaped = projected.reshape(3, images, length, local_heads, head_size)
    queries = shaped[0]
    keys_all = shaped[1]
    values_all = shaped[2]
    size_bias = jnp.log(sizes)[:, None, None, :]
    block = min(512, length)
    outputs = []
    for begin in range(0, length, block):
        scores = (
            jnp.einsum(
                "iqhe,ikhe->ihqk",
                queries[:, begin : begin + block],
                keys_all,
                preferred_element_type=jnp.float32,
            )
            / math.sqrt(head_size)
            + size_bias
        )
        weights = jax.nn.softmax(scores, axis=-1).astype(jnp.bfloat16)
        attended_block = jnp.einsum(
            "ihqk,ikhe->iqhe", weights, values_all, preferred_element_type=jnp.float32
        )
        outputs.append(attended_block.astype(jnp.bfloat16).reshape(images, block, local_width))
    attended = jnp.concatenate(outputs, axis=1)
    branch = jnp.einsum(
        "ind,de->ine",
        attended,
        lax.all_gather(proj_weight, "dp", axis=1, tiled=True),
        preferred_element_type=jnp.float32,
    )
    weighted = sizes[:, :, None] * branch
    own_sizes = lax.dynamic_slice_in_dim(sizes, own_start, own_tokens, 1)
    own_weighted = own_sizes[:, :, None] * base
    local_total = lax.dynamic_update_slice_in_dim(
        weighted,
        lax.dynamic_slice_in_dim(weighted, own_start, own_tokens, 1) + own_weighted,
        own_start,
        1,
    )
    merged_count = kept_total // devices_mp
    own_order = lax.dynamic_slice_in_dim(
        kept_order, lax.axis_index("mp") * merged_count, merged_count, 1
    )
    scattered = lax.psum_scatter(
        jnp.transpose(
            merge_rows(local_total, kept_order, pair_source, pair_target), (1, 0, 2)
        ).astype(jnp.bfloat16),
        "mp",
        scatter_dimension=0,
        tiled=True,
    ).astype(jnp.float32)
    numerator = jnp.transpose(scattered, (1, 0, 2))
    merged_size = merge_rows(sizes[:, :, None], own_order, pair_source, pair_target)
    merged = numerator / merged_size
    normed_two = layer_norm(merged, ln2_gain).astype(jnp.bfloat16)
    gathered = lax.all_gather(normed_two, "mp", axis=1, tiled=True)
    columns = gathered
    hidden_sum = jnp.einsum(
        "imd,df->imf",
        columns,
        lax.all_gather(fc1_weight, "dp", axis=0, tiled=True),
        preferred_element_type=jnp.float32,
    )
    hidden = jax.nn.gelu(hidden_sum + fc1_bias).astype(jnp.bfloat16)
    partial_out = jnp.einsum(
        "imf,fd->imd",
        hidden,
        lax.all_gather(fc2_weight, "dp", axis=1, tiled=True),
        preferred_element_type=jnp.float32,
    )
    mlp_part = lax.psum_scatter(
        partial_out.astype(jnp.bfloat16), "mp", scatter_dimension=1, tiled=True
    ).astype(jnp.float32)
    return (merged + mlp_part).astype(jnp.bfloat16)


def solution(mesh):
    return jax.shard_map(
        shards,
        mesh=mesh,
        in_specs=(
            P("dp", "mp", None),
            P("dp", None),
            P(),
            P(None, "dp", "mp"),
            P("mp", "dp"),
            P(),
            P("dp", "mp"),
            P("mp"),
            P("mp", "dp"),
            P("dp", None),
            P("dp", None),
            P("dp", None),
        ),
        out_specs=P("dp", "mp", None),
        check_vma=False,
    )
```

profile of v0, /device:TPU:1, one launch (start us, length us, event | category | flops | bytes accessed | tf_op | source)
XLA Modules:
  0.0 317.7 jit_solution(4380768634615341311)
XLA Ops:
  6.6 1.3 convert_reduce_fusion
  7.9 1.4 fusion.30
  9.3 2.2 fusion.32
  13.8 28.3 %all_gather.20 = bf16[320,1280]{0,1:T(8,128)(2,1)S(1)} all-gather(bf16[320,160]{0,1:T(8,128)(2,1)S(1)} %copy-done.2), channel_id=1, replica_groups=mesh['dp'=8,'mp'=4] {'dp'}, dimensions={1}, use_global_device_ids=true | all-gather | bytes 921600 | tf_op jit(solution)/shard_map/all_gather | solution.py:85
  42.8 1.4 gather_fusion.2
  44.4 53.4 %all-gather.8.cloned.1.call-done = bf16[3,1280,320]{2,1,0:T(8,128)(2,1)} async-done(((bf16[3,160,320]{2,1,0:T(8,128)(2,1)}), bf16[3,1280,320]{2,1,0:T(8,128)(2,1)}) %all-gather.8.cloned.1.call-update) | async-done | bytes 2457616 | tf_op jit(solution)/shard_map/all_gather | solution.py:54
  97.8 5.4 %convert_bitcast_fusion = bf16[3,1,1024,320]{2,3,0,1:T(8,128)(2,1)S(1)} fusion(bf16[3,1280,320]{2,1,0:T(8,128)(2,1)} %all-gather.8.cloned.1.call-done, bf16[1,1024,1280]{2,1,0:T(8,128)(2,1)} %all-gather.6.cloned.1.call-done), kind=kOutput, calls=%fused_computation.38 | convolution fusion | flops 2517565440 | bytes 7045120 | tf_op jit(solution)/shard_map/ind,cdf->cinf/dot_general | solution.py:51
  103.3 4.9 %fusion.80 = (f32[4,512]{1,0:T(4,128)S(1)}, f32[4,512,1024]{2,1,0:T(8,128)}) fusion(f32[1024]{0:T(1024)S(1)} %bitcast.179, bf16[1024,4,80]{0,2,1:T(8,128)(2,1)S(1)} %bitcast.170, bf16[1,1024,4,80]{1,3,2,0:T(8,128)(2,1)S(1)} %bitcast.168), kind=kOutput, calls=%fused_computation.120 | convolution fusion | flops 343933952 | bytes 9383936 | tf_op jit(solution)/shard_map/sub | solution.py:76
  108.2 4.9 %fusion.79 = (f32[4,512]{1,0:T(4,128)S(1)}, f32[4,512,1024]{2,1,0:T(8,128)}) fusion(f32[1024]{0:T(1024)S(1)} %bitcast.180, bf16[1024,4,80]{0,2,1:T(8,128)(2,1)S(1)} %bitcast.171, bf16[1,1024,4,80]{1,3,2,0:T(8,128)(2,1)S(1)} %bitcast.169), kind=kOutput, calls=%fused_computation.119 | convolution fusion | flops 343933952 | bytes 9383936 | tf_op jit(solution)/shard_map/sub | solution.py:76
  113.0 5.1 %fusion.37 = bf16[4,80,512]{2,1,0:T(8,128)(2,1)S(1)} fusion(bf16[1024,4,80]{0,2,1:T(8,128)(2,1)S(1)} %bitcast.166, f32[4,512,1024]{2,1,0:T(8,128)} %get-tuple-element.13, f32[4,512]{1,0:T(4,128)S(1)} %get-tuple-element.12), kind=kOutput, calls=%fused_computation.55 | convolution fusion | flops 339902464 | bytes 9379840 | tf_op jit(solution)/shard_map/ihqk,ikhe->iqhe/dot_general | solution.py:77
  118.9 1.7 fusion.36
  120.6 4.0 %convolution_multiply_fusion = f32[1024,1280]{1,0:T(8,128)} fusion(bf16[320,1280]{0,1:T(8,128)(2,1)S(1)} %all_gather.20, f32[1024]{0:T(1024)S(1)} %bitcast.165, bf16[1,512,320]{1,2,0:T(8,128)(2,1)S(1)} %bitcast.173, bf16[1,512,320]{1,2,0:T(8,128)(2,1)S(1)} %bitcast.172), kind=kOutput, calls=%fused_computation.24 | convolution fusion | flops 841482240 | bytes 6721536 | tf_op jit(solution)/shard_map/ind,de->ine/dot_general | solution.py:82
  124.6 1.4 constant_dynamic-slice_fusion.2
  127.3 3.1 gather_fusion.1
  130.5 9.7 %gather_fusion = f32[1008,1280]{1,0:T(8,128)} fusion(f32[1024,1280]{1,0:T(8,128)} %fusion.35, s32[1024]{0:T(1024)S(1)} %pad_clamp_fusion.2), kind=kCustom, calls=%fused_computation | custom fusion | bytes 10325952 | tf_op jit(solution)/shard_map/jit(take_along_axis)/gather | solution.py:18
  140.1 5.1 %fusion.21 = bf16[1008,1,1280]{2,0,1:T(8,128)(2,1)S(1)} fusion(f32[1008,1280]{1,0:T(8,128)} %gather_fusion, pred[1008]{0:T(1024)(128)(4,1)S(1)} %compare_and_fusion, f32[16,1280]{1,0:T(8,128)S(1)} %gather_fusion.1, pred[16]{0:T(512)(128)(4,1)S(1)} %compare_and_fusion.1, s32[1008]{0:T(1024)S(1)} %bitcast.175, s32[16]{0:T(128)S(1)} %bitcast.185), kind=kOutput, calls=%fused_computation.33 | convolution fusion | flops 251633408 | bytes 7828480 | tf_op jit(solution)/shard_map/icr,ird->icd/dot_general | solution.py:21
  145.2 27.6 %fusion = bf16[256,1280]{1,0:T(8,128)(2,1)S(1)} fusion(bf16[1008,1,1280]{2,0,1:T(8,128)(2,1)S(1)} %fusion.21), kind=kCustom, calls=%all-reduce-scatter | all-reduce-scatter fusion | flops 1310721 | bytes 3236352
  172.8 4.4 %collective-permute-start = (bf16[12,1280]{1,0:T(8,128)(2,1)S(1)}, bf16[12,1280]{1,0:T(8,128)(2,1)S(1)}, u32[]{:S(2)}, u32[]{:S(2)}) collective-permute-start(bf16[12,1280]{1,0:T(8,128)(2,1)S(1)} %slice.36), channel_id=1, source_target_pairs={{0,1},{1,2},{2,3},{4,5},{5,6},{6,7},{8,9},{9,10},{10,11},{12,13},{... | collective-permute-start | bytes 92168
  180.9 2.1 copy.14
  183.1 39.2 %all-gather.14.cloned.1.call-done = bf16[1280,1280]{0,1:T(8,128)(2,1)} async-done(((bf16[1280,160]{0,1:T(8,128)(2,1)}), bf16[1280,1280]{0,1:T(8,128)(2,1)}) %all-gather.14.cloned.1.call-update) | async-done | bytes 3276816 | tf_op jit(solution)/shard_map/all_gather | solution.py:125
  222.2 42.2 %all-gather.10.cloned.1.call-done = bf16[1,1008,1280]{2,0,1:T(2,128)(2,1)} async-done(((bf16[1,252,1280]{2,0,1:T(2,128)(2,1)}), bf16[1,1008,1280]{2,0,1:T(2,128)(2,1)}) %all-gather.10.cloned.1.call-update) | async-done | bytes 2580496 | tf_op jit(solution)/shard_map/all_gather | solution.py:113
  264.5 12.8 %fusion.20 = bf16[1,1008,1280]{2,1,0:T(8,128)(2,1)} fusion(bf16[1280,1280]{0,1:T(8,128)(2,1)} %all-gather.14.cloned.1.call-done, bf16[1280,1280]{1,0:T(8,128)(2,1)} %all-gather.12.cloned.1.call-done, bf16[1,1008,1280]{2,0,1:T(2,128)(2,1)} %all-gather.10.cloned.1.call-done, f32[1280]{0:T(1024)S(1)} %copy-done.7), kind=kOutput, calls=%fused_computation.32 | convolution fusion | flops 6620221440 | bytes 11719680 | tf_op jit(solution)/shard_map/imf,fd->imd/dot_general | solution.py:122
  277.3 26.0 %fusion.1 = bf16[256,1280]{1,0:T(8,128)(2,1)S(1)} fusion(bf16[1,1008,1280]{2,1,0:T(8,128)(2,1)} %fusion.20), kind=kCustom, calls=%all-reduce-scatter.1 | all-reduce-scatter fusion | flops 1310721 | bytes 3236352
  303.4 4.4 %collective-permute-start.1 = (bf16[12,1280]{1,0:T(8,128)(2,1)S(1)}, bf16[12,1280]{1,0:T(8,128)(2,1)S(1)}, u32[]{:S(2)}, u32[]{:S(2)}) collective-permute-start(bf16[12,1280]{1,0:T(8,128)(2,1)S(1)} %slice.37), channel_id=1, source_target_pairs={{0,1},{1,2},{2,3},{4,5},{5,6},{6,7},{8,9},{9,10},{10,11},{12,13},{... | collective-permute-start | bytes 92168
  (62 shorter events, 11.8 us)
Async XLA Ops:
  6.5 7.1 %copy-start.8 = (s32[1,16]{1,0:T(1,128)S(1)}, s32[1,16]{1,0:T(1,128)}, u32[]{:S(2)}) copy-start(s32[1,16]{1,0:T(1,128)} %param.21) | copy-start | bytes 196
  6.5 7.2 %copy-start = (f32[1,1024]{1,0:T(1,128)S(1)}, f32[1,1024]{1,0:T(1,128)}, u32[]{:S(2)}) copy-start(f32[1,1024]{1,0:T(1,128)} %param.13) | copy-start | bytes 12292
  6.5 7.2 %copy-start.2 = (bf16[320,160]{0,1:T(8,128)(2,1)S(1)}, bf16[320,160]{0,1:T(8,128)(2,1)}, u32[]{:S(2)}) copy-start(bf16[320,160]{0,1:T(8,128)(2,1)} %param.16) | copy-start | bytes 307204
  6.5 35.5 %copy-start.3 = (s32[1,1008]{1,0:T(1,128)S(1)}, s32[1,1008]{1,0:T(1,128)}, u32[]{:S(2)}) copy-start(s32[1,1008]{1,0:T(1,128)} %param.23) | copy-start | bytes 12100
  6.5 37.8 %all-gather.6.cloned.1.call-start = ((), (), s32[]{:S(2)}) async-start(), calls=%async_computation | async-start | bytes 3276800 | tf_op jit(solution)/shard_map/all_gather | solution.py:48
  7.9 36.3 %copy-start.5 = (s32[1,16]{1,0:T(1,128)S(1)}, s32[1,16]{1,0:T(1,128)}, u32[]{:S(2)}) copy-start(s32[1,16]{1,0:T(1,128)} %param.22) | copy-start | bytes 196
  11.6 86.2 %all-gather.8.cloned.1.call-start = ((), (), s32[]{:S(2)}) async-start(), calls=%async_computation.1 | async-start | bytes 3317760 | tf_op jit(solution)/shard_map/all_gather | solution.py:54
  12.3 170.7 %all-gather.12.cloned.1.call-start = ((), (), s32[]{:S(2)}) async-start(), calls=%async_computation.3 | async-start | bytes 3686400 | tf_op jit(solution)/shard_map/all_gather | solution.py:118
  13.0 209.2 %all-gather.14.cloned.1.call-start = ((), (), s32[]{:S(2)}) async-start(), calls=%async_computation.4 | async-start | bytes 3686400 | tf_op jit(solution)/shard_map/all_gather | solution.py:125
  13.6 250.8 %all-gather.10.cloned.1.call-start = ((), (), s32[]{:S(2)}) async-start(), calls=%async_computation.2 | async-start | bytes 6451200 | tf_op jit(solution)/shard_map/all_gather | solution.py:113
  113.0 5.9 %copy-start.9 = (f32[4,512,1024]{2,1,0:T(8,128)S(1)}, f32[4,512,1024]{2,1,0:T(8,128)}, u32[]{:S(2)}) copy-start(f32[4,512,1024]{2,1,0:T(8,128)} %get-tuple-element.11) | copy-start | bytes 25165828
  120.6 5.4 %copy-start.1 = (bf16[1,256,1280]{2,1,0:T(8,128)(2,1)S(1)}, bf16[1,256,1280]{2,1,0:T(8,128)(2,1)}, u32[]{:S(2)}) copy-start(bf16[1,256,1280]{2,1,0:T(8,128)(2,1)} %param.12) | copy-start | bytes 1966084
  145.2 32.0 %copy-start.6 = (u32[32]{0:T(128)S(1)}, u32[32]{0:T(128)}, u32[]{:S(2)}) copy-start(u32[32]{0:T(128)} %constant.99) | copy-start | bytes 388
  145.2 35.3 %copy-start.4 = (f32[1280]{0:T(1024)S(1)}, f32[1280]{0:T(1024)}, u32[]{:S(2)}) copy-start(f32[1280]{0:T(1024)} %param.17) | copy-start | bytes 15364
  172.8 5.7 %collective-permute-start = (bf16[12,1280]{1,0:T(8,128)(2,1)S(1)}, bf16[12,1280]{1,0:T(8,128)(2,1)S(1)}, u32[]{:S(2)}, u32[]{:S(2)}) collective-permute-start(bf16[12,1280]{1,0:T(8,128)(2,1)S(1)} %slice.36), channel_id=1, source_target_pairs={{0,1},{1,2},{2,3},{4,5},{5,6},{6,7},{8,9},{9,10},{10,11},{12,13},{... | collective-permute-start | bytes 92168
  179.6 84.9 %copy-start.7 = (f32[1280]{0:T(1024)S(1)}, f32[1280]{0:T(1024)}, u32[]{:S(2)}) copy-start(f32[1280]{0:T(1024)} %param.19) | copy-start | bytes 15364
  303.4 5.5 %collective-permute-start.1 = (bf16[12,1280]{1,0:T(8,128)(2,1)S(1)}, bf16[12,1280]{1,0:T(8,128)(2,1)S(1)}, u32[]{:S(2)}, u32[]{:S(2)}) collective-permute-start(bf16[12,1280]{1,0:T(8,128)(2,1)S(1)} %slice.37), channel_id=1, source_target_pairs={{0,1},{1,2},{2,3},{4,5},{5,6},{6,7},{8,9},{9,10},{10,11},{12,13},{... | collective-permute-start | bytes 92168
Sparse Core Ops, SparseCore 0:
  11.7 27.9 all-gather.5
  41.9 55.8 all-gather.7
  100.0 59.9 all-gather.11
  162.0 60.1 all-gather.13
  223.6 40.7 all-gather.9
where the time goes:
time: 318 us
  waiting for transfers between devices  138 us (43%)
  blocking collectives  81.9 us (26%)
  matrix products  44 us (14%)
  local copies, waits for them, and re-layouts  22 us (7%)
  between operations  14.1 us (4%)
  starting transfers between devices  8.96 us (3%)
  other arithmetic  8.93 us (3%)
    unnamed x2, blocking collectives  53.6 us
    all_gather x1, waiting for transfers between devices, shards(): lax.all_gather(qkv_weight, 'dp', axis=1, tiled=True)  53.4 us
    all_gather x1, waiting for transfers between devices, shards(): gathered = lax.all_gather(normed_two, 'mp', axis=1, tiled=True)  42.2 us
    all_gather x1, waiting for transfers between devices, shards(): lax.all_gather(fc2_weight, 'dp', axis=1, tiled=True)  39.2 us
    all_gather x1, blocking collectives, shards(): lax.all_gather(proj_weight, 'dp', axis=1, tiled=True)  28.3 us
    dot_general x1, matrix products, shards(): jnp.einsum('imf,fd->imd', hidden, lax.all_gather(fc2_weight, 'dp', axis=1...  12.8 us
    gather x2, local copies, waits for them, and re-layouts, merge_rows(): kept_rows = jnp.take_along_axis(total, order_rows[:, :, None], axis=1)  11 us
    sub x2, matrix products, shards(): weights = jax.nn.softmax(scores, axis=-1).astype(jnp.bfloat16)  9.7 us
  transfers between devices with their start and end apart: 7, of which 4 were waited for; matrix products, arithmetic and copies ran while one was open for 26% of the time, Pallas kernels for 0%

commit v1 on v0

--- a/solution.py
+++ b/solution.py
@@ -6,6 +6,22 @@
 
 D = 1280
 HEADS = 16
+
+
+def ring_product(array, axis, dim, term):
+    size, mine, rows = (lax.axis_size(axis), lax.axis_index(axis), array.shape[dim])
+    right = [(i, (i + 1) % size) for i in range(size)]
+    left = [(i, (i - 1) % size) for i in range(size)]
+    half = size // 2
+    from_left = from_right = array
+    total = term(array, mine * rows)
+    for hop in range(1, half + 1):
+        from_left = lax.ppermute(from_left, axis, right)
+        if hop < size - half:
+            from_right = lax.ppermute(from_right, axis, left)
+            total = total + term(from_right, (mine + hop) % size * rows)
+        total = total + term(from_left, (mine - hop) % size * rows)
+    return total
 
 
 def layer_norm(values, gain):
@@ -48,11 +64,16 @@
     whole = lax.all_gather(normed, "mp", axis=1, tiled=True)
     local_width = qkv_weight.shape[2]
     columns = whole
-    projected = jnp.einsum(
-        "ind,cdf->cinf",
-        columns,
-        lax.all_gather(qkv_weight, "dp", axis=1, tiled=True),
-        preferred_element_type=jnp.float32,
+    projected = ring_product(
+        qkv_weight,
+        "dp",
+        1,
+        lambda own_block, at: jnp.einsum(
+            "ind,cdf->cinf",
+            lax.dynamic_slice_in_dim(columns, at, own_block.shape[1], axis=2),
+            own_block,
+            preferred_element_type=jnp.float32,
+        ),
     ).astype(jnp.bfloat16)
     local_heads = local_width // head_size
     shaped = projected.reshape(3, images, length, local_heads, head_size)

time: 318 us -> 307 us (0.965)
  waiting for transfers between devices: 138 us -> 77.6 us
  starting transfers between devices: 8.96 us -> 25.1 us
  blocking collectives: 81.9 us -> 97.4 us
  matrix products: 44 us -> 59 us
    all_gather x1 -> x0, waiting for transfers between devices: 53.4 us -> none  [shards(): lax.all_gather(qkv_weight, 'dp', axis=1, tiled=True)]
    all_gather x1, waiting for transfers between devices: 39.2 us -> 0.02 us  [shards(): lax.all_gather(fc2_weight, 'dp', axis=1, tiled=True)]
    ppermute x0 -> x7, waiting for transfers between devices: none -> 35.9 us  [the longest x4 21.1 us: ring_product(): from_left = lax.ppermute(from_left, axis, right)]
    ppermute x0 -> x7, starting transfers between devices: none -> 16.1 us  [the longest x3 9.61 us: ring_product(): from_right = lax.ppermute(from_right, axis, left)]
    dot_general x1 -> x8, matrix products: 5.38 us -> 20 us  [shards(): jnp.einsum('ind,cdf->cinf', lax.dynamic_slice_in_dim(columns, at, own_blo...]
    all_gather x1, blocking collectives: 28.3 us -> 39 us  [shards(): lax.all_gather(proj_weight, 'dp', axis=1, tiled=True)]
    unnamed x2, blocking collectives: 53.6 us -> 58.4 us
  transfers between devices with their start and end apart: 7 -> 13, of which waited for: 4 -> 5; matrix products, arithmetic and copies ran while one was open for 26% -> 34% of each run, Pallas kernels for 0% -> 0%
where the time goes in v1:
time: 307 us; the launch traced here: 306 us
  blocking collectives  97.4 us (32%)
  waiting for transfers between devices  77.6 us (25%)
  matrix products  59 us (19%)
  starting transfers between devices  25.1 us (8%)
  local copies, waits for them, and re-layouts  23.9 us (8%)
  between operations  14.4 us (5%)
  other arithmetic  8.89 us (3%)
    unnamed x2, blocking collectives  58.4 us
    all_gather x1, waiting for transfers between devices, shards(): gathered = lax.all_gather(normed_two, 'mp', axis=1, tiled=True)  39.8 us
    all_gather x1, blocking collectives, shards(): lax.all_gather(proj_weight, 'dp', axis=1, tiled=True)  39 us
    ppermute x4, waiting for transfers between devices, ring_product(): from_left = lax.ppermute(from_left, axis, right)  21.1 us
    dot_general x8, matrix products, shards(): jnp.einsum('ind,cdf->cinf', lax.dynamic_slice_in_dim(columns, at, own_blo...  20 us
    ppermute x3, waiting for transfers between devices, ring_product(): from_right = lax.ppermute(from_right, axis, left)  14.8 us
    dot_general x1, matrix products, shards(): jnp.einsum('imf,fd->imd', hidden, lax.all_gather(fc2_weight, 'dp', axis=1...  12.9 us
    gather x2, local copies, waits for them, and re-layouts, merge_rows(): kept_rows = jnp.take_along_axis(total, order_rows[:, :, None], axis=1)  10.9 us
  transfers between devices with their start and end apart: 13, of which 5 were waited for; matrix products, arithmetic and copies ran while one was open for 34% of the time, Pallas kernels for 0%

profile of v1, /device:TPU:1, one launch (start us, length us, event | category | flops | bytes accessed | tf_op | source)
XLA Modules:
  0.0 306.2 jit_solution(3818731294387938143)
XLA Ops:
  14.5 3.1 %collective-permute-start = (bf16[3,160,320]{2,1,0:T(8,128)(2,1)}, bf16[3,160,320]{2,1,0:T(8,128)(2,1)S(1)}, u32[]{:S(2)}, u32[]{:S(2)}) collective-permute-start(bf16[3,160,320]{2,1,0:T(8,128)(2,1)} %param.15), channel_id=1, source_target_pairs={{0,28},{4,0},{8,4},{12,8},{16,12},{20,16},{24,20},{28,24},{1,29},{... | collective-permute-start | bytes 921608 | tf_op jit(solution)/shard_map/ppermute | solution.py:21
  20.3 9.7 %collective-permute-done.1 = bf16[3,160,320]{2,1,0:T(8,128)(2,1)S(1)} collective-permute-done((bf16[3,160,320]{2,1,0:T(8,128)(2,1)}, bf16[3,160,320]{2,1,0:T(8,128)(2,1)S(1)}, u32[]{:S(2)}, u32[]{:S(2)}) %collective-permute-start.1) | collective-permute-done | bytes 307232 | tf_op jit(solution)/shard_map/ppermute | solution.py:19
  32.2 3.1 %collective-permute-start.2 = (bf16[3,160,320]{2,1,0:T(8,128)(2,1)S(1)}, bf16[3,160,320]{2,1,0:T(8,128)(2,1)}, u32[]{:S(2)}, u32[]{:S(2)}) collective-permute-start(bf16[3,160,320]{2,1,0:T(8,128)(2,1)S(1)} %collective-permute-done), channel_id=1, source_target_pairs={{0,28},{4,0},{8,4},{12,8},{16,12},{20,16},{24,20},{28,24},{1,29},{... | collective-permute-start | bytes 921608 | tf_op jit(solution)/shard_map/ppermute | solution.py:21
  35.3 11.4 %collective-permute-done.3 = bf16[3,160,320]{2,1,0:T(8,128)(2,1)S(1)} collective-permute-done((bf16[3,160,320]{2,1,0:T(8,128)(2,1)S(1)}, bf16[3,160,320]{2,1,0:T(8,128)(2,1)S(1)}, u32[]{:S(2)}, u32[]{:S(2)}) %collective-permute-start.3) | collective-permute-done | bytes 307232 | tf_op jit(solution)/shard_map/ppermute | solution.py:19
  48.9 39.0 %all_gather.16 = bf16[320,1280]{0,1:T(8,128)(2,1)S(1)} all-gather(bf16[320,160]{0,1:T(8,128)(2,1)S(1)} %copy-done.6), channel_id=1, replica_groups=mesh['dp'=8,'mp'=4] {'dp'}, dimensions={1}, use_global_device_ids=true | all-gather | bytes 921600 | tf_op jit(solution)/shard_map/all_gather | solution.py:106
  87.9 3.4 %collective-permute-start.4 = (bf16[3,160,320]{2,1,0:T(8,128)(2,1)}, bf16[3,160,320]{2,1,0:T(8,128)(2,1)}, u32[]{:S(2)}, u32[]{:S(2)}) collective-permute-start(bf16[3,160,320]{2,1,0:T(8,128)(2,1)} %collective-permute-done.2), channel_id=1, source_target_pairs={{0,28},{4,0},{8,4},{12,8},{16,12},{20,16},{24,20},{28,24},{1,29},{... | collective-permute-start | bytes 921608 | tf_op jit(solution)/shard_map/ppermute | solution.py:21
  91.3 2.2 fusion.45
  98.0 2.7 fusion.57
  100.7 14.8 %collective-permute-done.4 = bf16[3,160,320]{2,1,0:T(8,128)(2,1)} collective-permute-done((bf16[3,160,320]{2,1,0:T(8,128)(2,1)}, bf16[3,160,320]{2,1,0:T(8,128)(2,1)}, u32[]{:S(2)}, u32[]{:S(2)}) %collective-permute-start.4) | collective-permute-done | bytes 307232 | tf_op jit(solution)/shard_map/ppermute | solution.py:21
  115.5 3.7 %fusion.47 = f32[1024,3,320]{0,2,1:T(8,128)} fusion(bf16[3,160,320]{2,1,0:T(8,128)(2,1)} %collective-permute-done.4, bf16[1,1024,1280]{2,1,0:T(8,128)(2,1)S(1)} %copy-done.2, s32[]{:T(128)S(6)} %select_n.215), kind=kOutput, calls=%fused_computation.65 | convolution fusion | flops 314572800 | bytes 4763652 | tf_op jit(solution)/shard_map/ind,cdf->cinf/dot_general | solution.py:71
  119.2 7.1 %fusion.24 = bf16[3,1,1024,320]{2,3,0,1:T(8,128)(2,1)} fusion(bf16[3,160,320]{2,1,0:T(8,128)(2,1)} %collective-permute-done.6, f32[1024,3,320]{0,2,1:T(8,128)S(1)} %fusion.45, f32[1024,3,320]{0,2,1:T(8,128)} %fusion.47, f32[1024,3,320]{0,2,1:T(8,128)S(1)} %fusion.49, f32[1024,3,320]{0,2,1:T(8,128)S(1)} %fusion.51, f32[1024,3,320]{0,2,1:T(8,128)S(1)} %fusion.53, ...), kind=kOutput, calls=%fused_computation.40 | convolution fusion | flops 322437120 | bytes 30384132 | tf_op jit(solution)/shard_map/ind,cdf->cinf/dot_general | solution.py:71
  127.9 5.0 %fusion.108 = (f32[4,512]{1,0:T(4,128)S(1)}, f32[4,512,1024]{2,1,0:T(8,128)}) fusion(f32[1024]{0:T(1024)S(1)} %bitcast.220, bf16[1024,4,80]{0,2,1:T(8,128)(2,1)S(1)} %bitcast.211, bf16[1,1024,4,80]{1,3,2,0:T(8,128)(2,1)S(1)} %bitcast.209), kind=kOutput, calls=%fused_computation.150 | convolution fusion | flops 343933952 | bytes 9383936 | tf_op jit(solution)/shard_map/sub | solution.py:97
  132.9 4.8 %fusion.107 = (f32[4,512]{1,0:T(4,128)S(1)}, f32[4,512,1024]{2,1,0:T(8,128)}) fusion(f32[1024]{0:T(1024)S(1)} %bitcast.221, bf16[1024,4,80]{0,2,1:T(8,128)(2,1)S(1)} %bitcast.212, bf16[1,1024,4,80]{1,3,2,0:T(8,128)(2,1)S(1)} %bitcast.210), kind=kOutput, calls=%fused_computation.149 | convolution fusion | flops 343933952 | bytes 9383936 | tf_op jit(solution)/shard_map/sub | solution.py:97
  137.7 5.0 %fusion.34 = bf16[4,80,512]{2,1,0:T(8,128)(2,1)S(1)} fusion(bf16[1024,4,80]{0,2,1:T(8,128)(2,1)S(1)} %bitcast.207, f32[4,512,1024]{2,1,0:T(8,128)} %get-tuple-element.13, f32[4,512]{1,0:T(4,128)S(1)} %get-tuple-element.12), kind=kOutput, calls=%fused_computation.54 | convolution fusion | flops 339902464 | bytes 9379840 | tf_op jit(solution)/shard_map/ihqk,ikhe->iqhe/dot_general | solution.py:98
  145.3 4.0 %convolution_multiply_fusion = f32[1024,1280]{1,0:T(8,128)} fusion(bf16[320,1280]{0,1:T(8,128)(2,1)S(1)} %all_gather.16, f32[1024]{0:T(1024)S(1)} %bitcast.206, bf16[1,512,320]{1,2,0:T(8,128)(2,1)S(1)} %bitcast.214, bf16[1,512,320]{1,2,0:T(8,128)(2,1)S(1)} %bitcast.213), kind=kOutput, calls=%fused_computation.24 | convolution fusion | flops 841482240 | bytes 6721536 | tf_op jit(solution)/shard_map/ind,de->ine/dot_general | solution.py:103
  152.0 3.1 %gather_fusion.1 = f32[16,1280]{1,0:T(8,128)S(1)} fusion(f32[1024,1280]{1,0:T(8,128)} %fusion.32, s32[1024]{0:T(1024)S(1)} %pad_clamp_fusion.1), kind=kCustom, calls=%fused_computation.1 | custom fusion | bytes 163904 | tf_op jit(solution)/shard_map/jit(take_along_axis)/gather | solution.py:35
  155.2 9.6 %gather_fusion = f32[1008,1280]{1,0:T(8,128)} fusion(f32[1024,1280]{1,0:T(8,128)} %fusion.32, s32[1024]{0:T(1024)S(1)} %pad_clamp_fusion.2), kind=kCustom, calls=%fused_computation | custom fusion | bytes 10325952 | tf_op jit(solution)/shard_map/jit(take_along_axis)/gather | solution.py:34
  164.7 5.5 %fusion.21 = bf16[1008,1,1280]{2,0,1:T(8,128)(2,1)S(1)} fusion(f32[1008,1280]{1,0:T(8,128)} %gather_fusion, pred[1008]{0:T(1024)(128)(4,1)S(1)} %compare_and_fusion, f32[16,1280]{1,0:T(8,128)S(1)} %gather_fusion.1, pred[16]{0:T(512)(128)(4,1)S(1)} %compare_and_fusion.1, s32[1008]{0:T(1024)S(1)} %bitcast.216, s32[16]{0:T(128)S(1)} %bitcast.226), kind=kOutput, calls=%fused_computation.34 | convolution fusion | flops 251633408 | bytes 7828480 | tf_op jit(solution)/shard_map/icr,ird->icd/dot_general | solution.py:37
  170.2 32.3 %fusion = bf16[256,1280]{1,0:T(8,128)(2,1)S(1)} fusion(bf16[1008,1,1280]{2,0,1:T(8,128)(2,1)S(1)} %fusion.21), kind=kCustom, calls=%all-reduce-scatter | all-reduce-scatter fusion | flops 1310721 | bytes 3236352
  202.6 4.4 %collective-permute-start.7 = (bf16[12,1280]{1,0:T(8,128)(2,1)S(1)}, bf16[12,1280]{1,0:T(8,128)(2,1)S(1)}, u32[]{:S(2)}, u32[]{:S(2)}) collective-permute-start(bf16[12,1280]{1,0:T(8,128)(2,1)S(1)} %slice.36), channel_id=1, source_target_pairs={{0,1},{1,2},{2,3},{4,5},{5,6},{6,7},{8,9},{9,10},{10,11},{12,13},{... | collective-permute-start | bytes 92168
  213.1 39.8 %all-gather.7.cloned.1.call-done = bf16[1,1008,1280]{2,0,1:T(2,128)(2,1)} async-done(((bf16[1,252,1280]{2,0,1:T(2,128)(2,1)}), bf16[1,1008,1280]{2,0,1:T(2,128)(2,1)}) %all-gather.7.cloned.1.call-update) | async-done | bytes 2580496 | tf_op jit(solution)/shard_map/all_gather | solution.py:134
  253.0 12.9 %fusion.20 = bf16[1,1008,1280]{2,1,0:T(8,128)(2,1)} fusion(bf16[1280,1280]{0,1:T(8,128)(2,1)} %all-gather.11.cloned.1.call-done, bf16[1280,1280]{1,0:T(8,128)(2,1)} %all-gather.9.cloned.1.call-done, bf16[1,1008,1280]{2,0,1:T(2,128)(2,1)} %all-gather.7.cloned.1.call-done, f32[1280]{0:T(1024)S(1)} %copy-done.11), kind=kOutput, calls=%fused_computation.33 | convolution fusion | flops 6620221440 | bytes 11719680 | tf_op jit(solution)/shard_map/imf,fd->imd/dot_general | solution.py:143
  265.8 26.0 %fusion.1 = bf16[256,1280]{1,0:T(8,128)(2,1)S(1)} fusion(bf16[1,1008,1280]{2,1,0:T(8,128)(2,1)} %fusion.20), kind=kCustom, calls=%all-reduce-scatter.1 | all-reduce-scatter fusion | flops 1310721 | bytes 3236352
  291.9 4.4 %collective-permute-start.8 = (bf16[12,1280]{1,0:T(8,128)(2,1)S(1)}, bf16[12,1280]{1,0:T(8,128)(2,1)S(1)}, u32[]{:S(2)}, u32[]{:S(2)}) collective-permute-start(bf16[12,1280]{1,0:T(8,128)(2,1)S(1)} %slice.37), channel_id=1, source_target_pairs={{0,1},{1,2},{2,3},{4,5},{5,6},{6,7},{8,9},{9,10},{10,11},{12,13},{... | collective-permute-start | bytes 92168
  (88 shorter events, 34.8 us)
Async XLA Ops:
  6.5 11.2 %copy-start.12 = (s32[1,16]{1,0:T(1,128)S(1)}, s32[1,16]{1,0:T(1,128)}, u32[]{:S(2)}) copy-start(s32[1,16]{1,0:T(1,128)} %param.21) | copy-start | bytes 196
  6.5 11.3 %copy-start = (f32[1,1024]{1,0:T(1,128)S(1)}, f32[1,1024]{1,0:T(1,128)}, u32[]{:S(2)}) copy-start(f32[1,1024]{1,0:T(1,128)} %param.13) | copy-start | bytes 12292
  6.5 11.3 %copy-start.7 = (s32[1,1008]{1,0:T(1,128)S(1)}, s32[1,1008]{1,0:T(1,128)}, u32[]{:S(2)}) copy-start(s32[1,1008]{1,0:T(1,128)} %param.23) | copy-start | bytes 12100
  6.5 13.5 %copy-start.9 = (s32[1,16]{1,0:T(1,128)S(1)}, s32[1,16]{1,0:T(1,128)}, u32[]{:S(2)}) copy-start(s32[1,16]{1,0:T(1,128)} %param.22) | copy-start | bytes 196
  6.5 42.3 %copy-start.6 = (bf16[320,160]{0,1:T(8,128)(2,1)S(1)}, bf16[320,160]{0,1:T(8,128)(2,1)}, u32[]{:S(2)}) copy-start(bf16[320,160]{0,1:T(8,128)(2,1)} %param.16) | copy-start | bytes 307204
  6.5 84.7 %all-gather.5.cloned.1.call-start = ((), (), s32[]{:S(2)}) async-start(), calls=%async_computation | async-start | bytes 3276800 | tf_op jit(solution)/shard_map/all_gather | solution.py:64
  11.6 201.5 %all-gather.11.cloned.1.call-start = ((), (), s32[]{:S(2)}) async-start(), calls=%async_computation.3 | async-start | bytes 3686400 | tf_op jit(solution)/shard_map/all_gather | solution.py:146
  12.3 200.8 %all-gather.9.cloned.1.call-start = ((), (), s32[]{:S(2)}) async-start(), calls=%async_computation.2 | async-start | bytes 3686400 | tf_op jit(solution)/shard_map/all_gather | solution.py:139
  12.4 17.6 %collective-permute-start.1 = (bf16[3,160,320]{2,1,0:T(8,128)(2,1)}, bf16[3,160,320]{2,1,0:T(8,128)(2,1)S(1)}, u32[]{:S(2)}, u32[]{:S(2)}) collective-permute-start(bf16[3,160,320]{2,1,0:T(8,128)(2,1)} %param.15), channel_id=1, source_target_pairs={{0,4},{4,8},{8,12},{12,16},{16,20},{20,24},{24,28},{28,0},{1,5},{5... | collective-permute-start | bytes 921608 | tf_op jit(solution)/shard_map/ppermute | solution.py:19
  14.5 17.7 %collective-permute-start = (bf16[3,160,320]{2,1,0:T(8,128)(2,1)}, bf16[3,160,320]{2,1,0:T(8,128)(2,1)S(1)}, u32[]{:S(2)}, u32[]{:S(2)}) collective-permute-start(bf16[3,160,320]{2,1,0:T(8,128)(2,1)} %param.15), channel_id=1, source_target_pairs={{0,28},{4,0},{8,4},{12,8},{16,12},{20,16},{24,20},{28,24},{1,29},{... | collective-permute-start | bytes 921608 | tf_op jit(solution)/shard_map/ppermute | solution.py:21
  17.6 235.4 %all-gather.7.cloned.1.call-start = ((), (), s32[]{:S(2)}) async-start(), calls=%async_computation.1 | async-start | bytes 6451200 | tf_op jit(solution)/shard_map/all_gather | solution.py:134
  30.0 16.7 %collective-permute-start.3 = (bf16[3,160,320]{2,1,0:T(8,128)(2,1)S(1)}, bf16[3,160,320]{2,1,0:T(8,128)(2,1)S(1)}, u32[]{:S(2)}, u32[]{:S(2)}) collective-permute-start(bf16[3,160,320]{2,1,0:T(8,128)(2,1)S(1)} %collective-permute-done.1), channel_id=1, source_target_pairs={{0,4},{4,8},{8,12},{12,16},{16,20},{20,24},{24,28},{28,0},{1,5},{5... | collective-permute-start | bytes 921608 | tf_op jit(solution)/shard_map/ppermute | solution.py:19
  32.2 62.2 %copy-start.4 = (bf16[3,160,320]{2,1,0:T(8,128)(2,1)}, bf16[3,160,320]{2,1,0:T(8,128)(2,1)S(1)}, u32[]{:S(2)}) copy-start(bf16[3,160,320]{2,1,0:T(8,128)(2,1)S(1)} %collective-permute-done) | copy-start | bytes 921604
  32.2 55.7 %collective-permute-start.2 = (bf16[3,160,320]{2,1,0:T(8,128)(2,1)S(1)}, bf16[3,160,320]{2,1,0:T(8,128)(2,1)}, u32[]{:S(2)}, u32[]{:S(2)}) collective-permute-start(bf16[3,160,320]{2,1,0:T(8,128)(2,1)S(1)} %collective-permute-done), channel_id=1, source_target_pairs={{0,28},{4,0},{8,4},{12,8},{16,12},{20,16},{24,20},{28,24},{1,29},{... | collective-permute-start | bytes 921608 | tf_op jit(solution)/shard_map/ppermute | solution.py:21
  46.7 44.6 %collective-permute-start.5 = (bf16[3,160,320]{2,1,0:T(8,128)(2,1)S(1)}, bf16[3,160,320]{2,1,0:T(8,128)(2,1)}, u32[]{:S(2)}, u32[]{:S(2)}) collective-permute-start(bf16[3,160,320]{2,1,0:T(8,128)(2,1)S(1)} %collective-permute-done.3), channel_id=1, source_target_pairs={{0,4},{4,8},{8,12},{12,16},{16,20},{20,24},{24,28},{28,0},{1,5},{5... | collective-permute-start | bytes 921608 | tf_op jit(solution)/shard_map/ppermute | solution.py:19
  87.9 27.6 %collective-permute-start.4 = (bf16[3,160,320]{2,1,0:T(8,128)(2,1)}, bf16[3,160,320]{2,1,0:T(8,128)(2,1)}, u32[]{:S(2)}, u32[]{:S(2)}) collective-permute-start(bf16[3,160,320]{2,1,0:T(8,128)(2,1)} %collective-permute-done.2), channel_id=1, source_target_pairs={{0,28},{4,0},{8,4},{12,8},{16,12},{20,16},{24,20},{28,24},{1,29},{... | collective-permute-start | bytes 921608 | tf_op jit(solution)/shard_map/ppermute | solution.py:21
  91.3 27.9 %collective-permute-start.6 = (bf16[3,160,320]{2,1,0:T(8,128)(2,1)}, bf16[3,160,320]{2,1,0:T(8,128)(2,1)}, u32[]{:S(2)}, u32[]{:S(2)}) collective-permute-start(bf16[3,160,320]{2,1,0:T(8,128)(2,1)} %collective-permute-done.5), channel_id=1, source_target_pairs={{0,4},{4,8},{8,12},{12,16},{16,20},{20,24},{24,28},{28,0},{1,5},{5... | collective-permute-start | bytes 921608 | tf_op jit(solution)/shard_map/ppermute | solution.py:19
  137.7 5.9 %copy-start.13 = (f32[4,512,1024]{2,1,0:T(8,128)S(1)}, f32[4,512,1024]{2,1,0:T(8,128)}, u32[]{:S(2)}) copy-start(f32[4,512,1024]{2,1,0:T(8,128)} %get-tuple-element.11) | copy-start | bytes 25165828
  145.3 5.4 %copy-start.1 = (bf16[1,256,1280]{2,1,0:T(8,128)(2,1)S(1)}, bf16[1,256,1280]{2,1,0:T(8,128)(2,1)}, u32[]{:S(2)}) copy-start(bf16[1,256,1280]{2,1,0:T(8,128)(2,1)} %param.12) | copy-start | bytes 1966084
  164.7 42.3 %copy-start.10 = (u32[32]{0:T(128)S(1)}, u32[32]{0:T(128)}, u32[]{:S(2)}) copy-start(u32[32]{0:T(128)} %constant.159) | copy-start | bytes 388
  170.2 40.3 %copy-start.8 = (f32[1280]{0:T(1024)S(1)}, f32[1280]{0:T(1024)}, u32[]{:S(2)}) copy-start(f32[1280]{0:T(1024)} %param.17) | copy-start | bytes 15364
  202.6 50.4 %copy-start.11 = (f32[1280]{0:T(1024)S(1)}, f32[1280]{0:T(1024)}, u32[]{:S(2)}) copy-start(f32[1280]{0:T(1024)} %param.19) | copy-start | bytes 15364
  202.6 5.7 %collective-permute-start.7 = (bf16[12,1280]{1,0:T(8,128)(2,1)S(1)}, bf16[12,1280]{1,0:T(8,128)(2,1)S(1)}, u32[]{:S(2)}, u32[]{:S(2)}) collective-permute-start(bf16[12,1280]{1,0:T(8,128)(2,1)S(1)} %slice.36), channel_id=1, source_target_pairs={{0,1},{1,2},{2,3},{4,5},{5,6},{6,7},{8,9},{9,10},{10,11},{12,13},{... | collective-permute-start | bytes 92168
  291.9 5.5 %collective-permute-start.8 = (bf16[12,1280]{1,0:T(8,128)(2,1)S(1)}, bf16[12,1280]{1,0:T(8,128)(2,1)S(1)}, u32[]{:S(2)}, u32[]{:S(2)}) collective-permute-start(bf16[12,1280]{1,0:T(8,128)(2,1)S(1)} %slice.37), channel_id=1, source_target_pairs={{0,1},{1,2},{2,3},{4,5},{5,6},{6,7},{8,9},{9,10},{10,11},{12,13},{... | collective-permute-start | bytes 92168
  (3 other events, 5.0 us)
Sparse Core Ops, SparseCore 0:
  11.7 27.9 all-gather.4
  41.9 91.1 all-gather.10
  135.3 59.7 all-gather.8
  213.2 39.7 all-gather.6
